TPU v7x, 32 devices: a whole 2x2x4 slice. The times are simulated.
32 devices in a mesh: wide: 8 (over z, core), narrow: 4 (over y, x).
Axes of the slice: x: 2, y: 2, z: 4, core: 2. Of those that a mesh axis runs over, the one named last changes fastest.
Arguments:
- tridiag_vectors: float32 [128, 131072], P(('wide', 'narrow')), may hold values from -6 to 6
- reflectors: float32 [2, 131072, 256], P(None, 'wide'), may hold values from -0.015625 to 0.015625
- triangles: float32 [2, 256, 256], replicated, as said below
- lower_blocks: float32 [6, 1536, 1536], P(None, 'wide'), may hold values from -0.109375 to 0.109375
- diag_inverses: float32 [4, 1536, 1536], P(None, None, 'wide'), as said below
Outputs:
- transformed: float32 [128, 131072], P('narrow', 'wide')
- solved: float32 [128, 4, 1536], P('narrow', None, 'wide')
Inputs may be any that keep to these rules, and one draw needn't show every extreme that they name: `triangles`: zero below the diagonal, positive on it. `diag_inverses`: zero above the diagonal, positive on it.
All inputs are finite; a program needn't handle non-finite values.
Results may differ from a plain program's by a relative error of at most 0.00019.
Values sent between devices are 32-bit elements; how exact they have to be, the bound alone decides.
A program may use at most 128 MiB of HBM per device.

v0:
```python
import jax
import jax.numpy as jnp
from jax import lax
from jax.sharding import PartitionSpec as P

HIGHEST = lax.Precision.HIGHEST


def reflect(current, vectors, factor, products):
    coeffs = jnp.dot(products, factor.T, precision=HIGHEST)
    return current - jnp.dot(coeffs, vectors.T, precision=HIGHEST)


def add_piece(inverse, segment):
    return jnp.dot(segment, inverse, precision=HIGHEST)


def solve_chain(corner, lower_blocks, diag_inverses):
    local_count, panels, share_cols = corner.shape
    zeroed = jnp.zeros((local_count, share_cols), jnp.float32)
    pending = [zeroed] * panels
    results = [zeroed] * panels
    for source in reversed(range(panels)):
        remain = corner[:, source, :] - pending[source]
        solution = add_piece(
            diag_inverses[source], lax.all_gather(remain, "wide", axis=1, tiled=True)
        )
        results[source] = solution
        if source > 0:
            offset = source * (source - 1) // 2
            blocks = lower_blocks[offset : offset + source]
            partial_terms = jnp.einsum("ks,qsc->kqc", solution, blocks, precision=HIGHEST)
            scattered = lax.psum_scatter(partial_terms, "wide", scatter_dimension=2, tiled=True)
            for target in range(source):
                pending[target] = pending[target] + scattered[:, target, :]
    return jnp.stack(results, axis=1)


def body(tridiag_vectors, reflectors, triangles, lower_blocks, diag_inverses):
    wide_size = lax.axis_size("wide")
    spread = lax.all_to_all(
        tridiag_vectors, ("wide", "narrow"), split_axis=1, concat_axis=0, tiled=True
    )
    current = lax.all_to_all(spread, "narrow", split_axis=0, concat_axis=1, tiled=True)
    for which in (1, 0):
        products = lax.psum(jnp.dot(current, reflectors[which], precision=HIGHEST), "wide")
        current = reflect(current, reflectors[which], triangles[which], products)
    panels, panel_rows, share_cols = diag_inverses.shape
    corner_span = panels * panel_rows
    tail_cols = current[:, current.shape[1] - corner_span :]
    framed = tail_cols.reshape(tail_cols.shape[0], panels, wide_size, share_cols)
    received = lax.all_to_all(framed, "wide", split_axis=2, concat_axis=2, tiled=True)
    corner = received[:, :, wide_size - 1, :]
    solved = solve_chain(corner, lower_blocks, diag_inverses)
    return (current, solved)


def solution(mesh):
    placed = (
        P(("wide", "narrow"), None),
        P(None, "wide", None),
        P(),
        P(None, "wide", None),
        P(None, None, "wide"),
    )
    return jax.shard_map(
        body,
        mesh=mesh,
        in_specs=placed,
        out_specs=(P("narrow", "wide"), P("narrow", None, "wide")),
        check_vma=False,
    )
```

profile of v0, /device:TPU:0, one launch (start us, length us, event | category | flops | bytes accessed | tf_op | source)
XLA Modules:
  0.0 433.0 jit_solution(8765695923981802089)
XLA Ops:
  7.2 56.5 %all_to_all.40 = f32[4,32,4096]{2,0,1:T(4,128)} all-to-all(f32[4,32,4096]{2,0,1:T(4,128)} %bitcast.93), channel_id=1, replica_groups=mesh['wide'=8,'narrow'=4] {'wide','narrow'}, dimensions={1} | all-to-all | bytes 4194304 | tf_op jit(solution)/shard_map/all_to_all | solution.py:41
  65.6 28.2 %all_to_all.41 = f32[4,32,4096]{2,1,0:T(8,128)S(1)} all-to-all(f32[4,32,4096]{2,1,0:T(8,128)S(1)} %all_to_all.32), channel_id=1, replica_groups=mesh['wide'=8,'narrow'=4] {'narrow'}, dimensions={0} | all-to-all | bytes 4194304 | tf_op jit(solution)/shard_map/all_to_all | solution.py:44
  95.3 10.7 %fusion.4 = f32[32,256]{1,0:T(8,128)S(1)} fusion(f32[32,16384]{1,0:T(8,128)S(1)} %bitcast.83, f32[2,16384,256]{2,1,0:T(8,128)} %param.6), kind=kOutput, calls=%fused_computation.6 | convolution fusion | flops 1610612736 | bytes 18907136 | tf_op jit(solution)/shard_map/dot_general | solution.py:46
  106.0 26.1 %psum.14 = f32[32,256]{1,0:T(8,128)S(1)} all-reduce(f32[32,256]{1,0:T(8,128)S(1)} %fusion.4), channel_id=1, replica_groups=mesh['wide'=8,'narrow'=4] {'wide'}, use_global_device_ids=true, to_apply=%region_0.0 | all-reduce | flops 8192 | bytes 65536 | tf_op jit(solution)/shard_map/psum | solution.py:46
  132.5 18.6 %convolution_subtract_fusion.1 = f32[32,16384]{1,0:T(8,128)S(1)} fusion(f32[32,16384]{1,0:T(8,128)} %bitcast.84, f32[32,256]{1,0:T(8,128)S(1)} %fusion.33, f32[2,16384,256]{2,1,0:T(8,128)} %param.6), kind=kOutput, calls=%fused_computation.1 | convolution fusion | flops 1611137024 | bytes 21004288 | tf_op jit(solution)/shard_map/dot_general | solution.py:11
  151.1 10.6 %fusion.1 = f32[32,256]{1,0:T(8,128)S(1)} fusion(f32[32,16384]{1,0:T(8,128)S(1)} %convolution_subtract_fusion.1, f32[2,16384,256]{2,1,0:T(8,128)} %param.6), kind=kOutput, calls=%fused_computation.3 | convolution fusion | flops 1610612736 | bytes 18907136 | tf_op jit(solution)/shard_map/dot_general | solution.py:46
  161.8 26.2 %psum.15 = f32[32,256]{1,0:T(8,128)S(1)} all-reduce(f32[32,256]{1,0:T(8,128)S(1)} %fusion.1), channel_id=1, replica_groups=mesh['wide'=8,'narrow'=4] {'wide'}, use_global_device_ids=true, to_apply=%region_1.0 | all-reduce | flops 8192 | bytes 65536 | tf_op jit(solution)/shard_map/psum | solution.py:46
  188.3 17.3 %convolution_subtract_fusion = f32[32,16384]{1,0:T(8,128)S(1)} fusion(f32[32,16384]{1,0:T(8,128)S(1)} %convolution_subtract_fusion.1, f32[32,256]{1,0:T(8,128)S(1)} %fusion.31, f32[2,16384,256]{2,1,0:T(8,128)} %param.6), kind=kOutput, calls=%fused_computation | convolution fusion | flops 1611137024 | bytes 21004288 | tf_op jit(solution)/shard_map/dot_general | solution.py:11
  208.0 29.0 %all_to_all.42 = f32[32,4,8,192]{3,0,1,2:T(8,128)S(1)} all-to-all(f32[32,4,8,192]{3,0,1,2:T(8,128)S(1)} %copy.22), channel_id=1, replica_groups=mesh['wide'=8,'narrow'=4] {'wide'}, dimensions={2} | all-to-all | bytes 1572864 | tf_op jit(solution)/shard_map/all_to_all | solution.py:52
  237.1 15.7 %all-gather = f32[32,1,1536]{0,1,2:T(1,128)S(1)} all-gather(f32[32,1,192]{0,1,2:T(1,128)S(1)} %copy.23), channel_id=2, replica_groups=mesh['wide'=8,'narrow'=4] {'wide'}, dimensions={2}, use_global_device_ids=true | all-gather | bytes 221184 | tf_op jit(solution)/shard_map/all_gather | solution.py:26
  252.9 2.6 fusion.21
  255.5 5.0 %fusion.10 = f32[32,3,1536]{2,0,1:T(8,128)} fusion(f32[6,192,1536]{2,1,0:T(8,128)} %param.8, f32[32,192]{1,0:T(8,128)S(1)} %fusion.21), kind=kOutput, calls=%fused_computation.12 | convolution fusion | flops 339738624 | bytes 4153344 | tf_op jit(solution)/shard_map/ks,qsc->kqc/dot_general | solution.py:32
  260.5 2.6 copy.28
  265.5 29.5 %reduce-scatter.10.cloned.1.call-done = f32[192,96]{1,0:T(8,128)} async-done(((f32[1536,96]{1,0:T(8,128)}), f32[192,96]{1,0:T(8,128)}) %reduce-scatter.10.cloned.1.call-update) | async-done | bytes 73744
  296.5 16.0 %all-gather.1 = f32[32,1,1536]{0,1,2:T(1,128)S(1)} all-gather(f32[32,1,192]{0,1,2:T(1,128)S(1)} %copy.24), channel_id=3, replica_groups=mesh['wide'=8,'narrow'=4] {'wide'}, dimensions={2}, use_global_device_ids=true | all-gather | bytes 221184 | tf_op jit(solution)/shard_map/all_gather | solution.py:26
  312.5 2.6 fusion.19
  315.1 3.2 fusion.12
  321.0 30.2 %reduce-scatter.12.cloned.1.call-done = f32[192,64]{1,0:T(8,128)} async-done(((f32[1536,64]{1,0:T(8,128)}), f32[192,64]{1,0:T(8,128)}) %reduce-scatter.12.cloned.1.call-update) | async-done | bytes 49168
  352.6 15.7 %all-gather.2 = f32[32,1,1536]{0,1,2:T(1,128)S(1)} all-gather(f32[32,1,192]{0,1,2:T(1,128)S(1)} %copy.25), channel_id=4, replica_groups=mesh['wide'=8,'narrow'=4] {'wide'}, dimensions={2}, use_global_device_ids=true | all-gather | bytes 221184 | tf_op jit(solution)/shard_map/all_gather | solution.py:26
  368.4 2.6 fusion.17
  371.0 4.8 %convolution_bitcast_fusion = f32[1536,32]{1,0:T(8,128)} fusion(f32[32,192]{1,0:T(8,128)S(1)} %fusion.17, f32[6,192,1536]{2,1,0:T(8,128)} %param.8), kind=kOutput, calls=%fused_computation.14 | convolution fusion | flops 113246208 | bytes 1400832 | tf_op jit(solution)/shard_map/ks,qsc->kqc/dot_general | solution.py:32
  375.9 30.3 %reduce-scatter.14.cloned.1.call-done = f32[192,32]{1,0:T(8,128)} async-done(((f32[1536,32]{1,0:T(8,128)}), f32[192,32]{1,0:T(8,128)}) %reduce-scatter.14.cloned.1.call-update) | async-done | bytes 24592
  407.3 15.7 %all-gather.3 = f32[32,1,1536]{0,1,2:T(1,128)S(1)} all-gather(f32[32,1,192]{0,1,2:T(1,128)S(1)} %copy.26), channel_id=5, replica_groups=mesh['wide'=8,'narrow'=4] {'wide'}, dimensions={2}, use_global_device_ids=true | all-gather | bytes 221184 | tf_op jit(solution)/shard_map/all_gather | solution.py:26
  423.1 2.6 fusion.28
  (43 shorter events, 16.5 us)
Async XLA Ops:
  7.2 287.9 %reduce-scatter.10.cloned.1.call-start = ((), (), s32[]{:S(2)}) async-start(), calls=%async_computation.6 | async-start | bytes 884736
  94.0 1.3 copy-start
  95.3 36.8 %copy-start.2 = (f32[2,256,256]{2,1,0:T(8,128)S(1)}, f32[2,256,256]{2,1,0:T(8,128)}, u32[]{:S(2)}) copy-start(f32[2,256,256]{2,1,0:T(8,128)} %param.7) | copy-start | bytes 1572868
  205.5 1.3 copy-start.1
  265.4 85.8 %reduce-scatter.12.cloned.1.call-start = ((), (), s32[]{:S(2)}) async-start(), calls=%async_computation.7 | async-start | bytes 884736
  320.9 85.4 %reduce-scatter.14.cloned.1.call-start = ((), (), s32[]{:S(2)}) async-start(), calls=%async_computation.8 | async-start | bytes 884736
Sparse Core Ops, SparseCore 0:
  265.6 29.4 reduce-scatter.9
  321.0 30.1 reduce-scatter.11
  375.9 30.2 reduce-scatter.13
where the time goes:
time: 434 us; the launch traced here: 433 us
  blocking collectives  229 us (53%)
  waiting for transfers between devices  90.1 us (21%)
  matrix products  81.5 us (19%)
  local copies, waits for them, and re-layouts  18.2 us (4%)
  between operations  14 us (3%)
    unnamed x6, waiting for transfers between devices  90.1 us
    all_gather x4, blocking collectives, solve_chain(): lax.all_gather(remain, 'wide', axis=1, tiled=True)  63.2 us
    all_to_all x1, blocking collectives, body(): lax.all_to_all(tridiag_vectors, ('wide', 'narrow'), split_axis=1, concat_...  56.5 us
    psum x2, blocking collectives, body(): lax.psum(jnp.dot(current, reflectors[which], precision=HIGHEST), 'wide')  52.3 us
    dot_general x2, matrix products, reflect(): return current - jnp.dot(coeffs, vectors.T, precision=HIGHEST)  35.9 us
    all_to_all x1, blocking collectives, body(): lax.all_to_all(framed, 'wide', split_axis=2, concat_axis=2, tiled=True)  29 us
    all_to_all x1, blocking collectives, body(): lax.all_to_all(spread, 'narrow', split_axis=0, concat_axis=1, tiled=True)  28.2 us
    dot_general x2, matrix products, body(): jnp.dot(current, reflectors[which], precision=HIGHEST)  21.3 us
  transfers between devices with their start and end apart: 3, of which 3 were waited for; matrix products, arithmetic and copies ran while one was open for 0% of the time, Pallas kernels for 0%

commit v1 on v0

--- a/solution.py
+++ b/solution.py
@@ -38,8 +38,16 @@
 
 def body(tridiag_vectors, reflectors, triangles, lower_blocks, diag_inverses):
     wide_size = lax.axis_size("wide")
-    spread = lax.all_to_all(
-        tridiag_vectors, ("wide", "narrow"), split_axis=1, concat_axis=0, tiled=True
+    spread = jnp.concatenate(
+        lax.all_to_all(
+            jnp.stack(
+                jnp.split(tridiag_vectors, lax.axis_size(("wide", "narrow")), axis=1), axis=0
+            ),
+            ("wide", "narrow"),
+            0,
+            0,
+        ),
+        axis=0,
     )
     current = lax.all_to_all(spread, "narrow", split_axis=0, concat_axis=1, tiled=True)
     for which in (1, 0):

time: 434 us -> 463 us (1.067)
  local copies, waits for them, and re-layouts: 18.2 us -> 45.2 us
    unnamed x19 -> x50, local copies, waits for them, and re-layouts: 14.2 us -> 40.6 us
where the time goes in v1:
time: 463 us; the launch traced here: 461 us
  blocking collectives  230 us (50%)
  waiting for transfers between devices  90 us (19%)
  matrix products  81.5 us (18%)
  local copies, waits for them, and re-layouts  45.2 us (10%)
  between operations  14 us (3%)
    unnamed x6, waiting for transfers between devices  90 us
    all_gather x4, blocking collectives, solve_chain(): lax.all_gather(remain, 'wide', axis=1, tiled=True)  63.2 us
    all_to_all x1, blocking collectives, body(): lax.all_to_all(jnp.stack(jnp.split(tridiag_vectors, lax.axis_size(('wide'...  56.1 us
    psum x2, blocking collectives, body(): lax.psum(jnp.dot(current, reflectors[which], precision=HIGHEST), 'wide')  52.3 us
    unnamed x50, local copies, waits for them, and re-layouts  40.6 us
    dot_general x2, matrix products, reflect(): return current - jnp.dot(coeffs, vectors.T, precision=HIGHEST)  35.9 us
    all_to_all x1, blocking collectives, body(): lax.all_to_all(spread, 'narrow', split_axis=0, concat_axis=1, tiled=True)  29.1 us
    all_to_all x1, blocking collectives, body(): lax.all_to_all(framed, 'wide', split_axis=2, concat_axis=2, tiled=True)  29 us
  transfers between devices with their start and end apart: 3, of which 3 were waited for; matrix products, arithmetic and copies ran while one was open for 0% of the time, Pallas kernels for 0%

profile of v1, /device:TPU:0, one launch (start us, length us, event | category | flops | bytes accessed | tf_op | source)
XLA Modules:
  0.0 460.5 jit_solution(985742255214312461)
XLA Ops:
  34.5 56.1 %all_to_all.29 = f32[32,4,4096]{2,1,0:T(4,128)S(1)} all-to-all(f32[32,4,4096]{2,1,0:T(4,128)S(1)} %constant_dynamic-update-slice_fusion), channel_id=1, replica_groups=mesh['wide'=8,'narrow'=4] {'wide','narrow'}, dimensions={0} | all-to-all | bytes 4194304 | tf_op jit(solution)/shard_map/all_to_all | solution.py:42
  92.4 29.1 %all_to_all.30 = f32[4,32,4096]{2,1,0:T(8,128)S(1)} all-to-all(f32[4,32,4096]{2,1,0:T(8,128)} %all_to_all.21), channel_id=1, replica_groups=mesh['wide'=8,'narrow'=4] {'narrow'}, dimensions={0} | all-to-all | bytes 4194304 | tf_op jit(solution)/shard_map/all_to_all | solution.py:52
  122.9 10.7 %fusion.4 = f32[32,256]{1,0:T(8,128)S(1)} fusion(f32[32,16384]{1,0:T(8,128)S(1)} %bitcast.145, f32[2,16384,256]{2,1,0:T(8,128)} %param.6), kind=kOutput, calls=%fused_computation.6 | convolution fusion | flops 1610612736 | bytes 18907136 | tf_op jit(solution)/shard_map/dot_general | solution.py:54
  133.6 26.2 %psum.14 = f32[32,256]{1,0:T(8,128)S(1)} all-reduce(f32[32,256]{1,0:T(8,128)S(1)} %fusion.4), channel_id=1, replica_groups=mesh['wide'=8,'narrow'=4] {'wide'}, use_global_device_ids=true, to_apply=%region_0.0 | all-reduce | flops 8192 | bytes 65536 | tf_op jit(solution)/shard_map/psum | solution.py:54
  160.1 18.6 %convolution_subtract_fusion.1 = f32[32,16384]{1,0:T(8,128)S(1)} fusion(f32[32,16384]{1,0:T(8,128)} %bitcast.146, f32[32,256]{1,0:T(8,128)S(1)} %fusion.33, f32[2,16384,256]{2,1,0:T(8,128)} %param.6), kind=kOutput, calls=%fused_computation.1 | convolution fusion | flops 1611137024 | bytes 21004288 | tf_op jit(solution)/shard_map/dot_general | solution.py:11
  178.8 10.6 %fusion.1 = f32[32,256]{1,0:T(8,128)S(1)} fusion(f32[32,16384]{1,0:T(8,128)S(1)} %convolution_subtract_fusion.1, f32[2,16384,256]{2,1,0:T(8,128)} %param.6), kind=kOutput, calls=%fused_computation.3 | convolution fusion | flops 1610612736 | bytes 18907136 | tf_op jit(solution)/shard_map/dot_general | solution.py:54
  189.4 26.2 %psum.15 = f32[32,256]{1,0:T(8,128)S(1)} all-reduce(f32[32,256]{1,0:T(8,128)S(1)} %fusion.1), channel_id=1, replica_groups=mesh['wide'=8,'narrow'=4] {'wide'}, use_global_device_ids=true, to_apply=%region_1.0 | all-reduce | flops 8192 | bytes 65536 | tf_op jit(solution)/shard_map/psum | solution.py:54
  215.9 17.3 %convolution_subtract_fusion = f32[32,16384]{1,0:T(8,128)S(1)} fusion(f32[32,16384]{1,0:T(8,128)S(1)} %convolution_subtract_fusion.1, f32[32,256]{1,0:T(8,128)S(1)} %fusion.31, f32[2,16384,256]{2,1,0:T(8,128)} %param.6), kind=kOutput, calls=%fused_computation | convolution fusion | flops 1611137024 | bytes 21004288 | tf_op jit(solution)/shard_map/dot_general | solution.py:11
  235.7 29.0 %all_to_all.31 = f32[32,4,8,192]{3,0,1,2:T(8,128)S(1)} all-to-all(f32[32,4,8,192]{3,0,1,2:T(8,128)S(1)} %copy.17), channel_id=1, replica_groups=mesh['wide'=8,'narrow'=4] {'wide'}, dimensions={2} | all-to-all | bytes 1572864 | tf_op jit(solution)/shard_map/all_to_all | solution.py:60
  264.8 15.7 %all-gather = f32[32,1,1536]{0,1,2:T(1,128)S(1)} all-gather(f32[32,1,192]{0,1,2:T(1,128)S(1)} %copy.18), channel_id=2, replica_groups=mesh['wide'=8,'narrow'=4] {'wide'}, dimensions={2}, use_global_device_ids=true | all-gather | bytes 221184 | tf_op jit(solution)/shard_map/all_gather | solution.py:26
  280.5 2.6 fusion.21
  283.2 5.0 %fusion.10 = f32[32,3,1536]{2,0,1:T(8,128)} fusion(f32[6,192,1536]{2,1,0:T(8,128)} %param.8, f32[32,192]{1,0:T(8,128)S(1)} %fusion.21), kind=kOutput, calls=%fused_computation.12 | convolution fusion | flops 339738624 | bytes 4153344 | tf_op jit(solution)/shard_map/ks,qsc->kqc/dot_general | solution.py:32
  288.2 2.6 copy.23
  293.2 29.4 %reduce-scatter.10.cloned.1.call-done = f32[192,96]{1,0:T(8,128)} async-done(((f32[1536,96]{1,0:T(8,128)}), f32[192,96]{1,0:T(8,128)}) %reduce-scatter.10.cloned.1.call-update) | async-done | bytes 73744
  324.1 16.0 %all-gather.1 = f32[32,1,1536]{0,1,2:T(1,128)S(1)} all-gather(f32[32,1,192]{0,1,2:T(1,128)S(1)} %copy.19), channel_id=3, replica_groups=mesh['wide'=8,'narrow'=4] {'wide'}, dimensions={2}, use_global_device_ids=true | all-gather | bytes 221184 | tf_op jit(solution)/shard_map/all_gather | solution.py:26
  340.1 2.6 fusion.19
  342.7 3.2 fusion.12
  348.6 30.2 %reduce-scatter.12.cloned.1.call-done = f32[192,64]{1,0:T(8,128)} async-done(((f32[1536,64]{1,0:T(8,128)}), f32[192,64]{1,0:T(8,128)}) %reduce-scatter.12.cloned.1.call-update) | async-done | bytes 49168
  380.2 15.7 %all-gather.2 = f32[32,1,1536]{0,1,2:T(1,128)S(1)} all-gather(f32[32,1,192]{0,1,2:T(1,128)S(1)} %copy.20), channel_id=4, replica_groups=mesh['wide'=8,'narrow'=4] {'wide'}, dimensions={2}, use_global_device_ids=true | all-gather | bytes 221184 | tf_op jit(solution)/shard_map/all_gather | solution.py:26
  395.9 2.6 fusion.17
  398.6 4.8 %convolution_bitcast_fusion = f32[1536,32]{1,0:T(8,128)} fusion(f32[32,192]{1,0:T(8,128)S(1)} %fusion.17, f32[6,192,1536]{2,1,0:T(8,128)} %param.8), kind=kOutput, calls=%fused_computation.14 | convolution fusion | flops 113246208 | bytes 1400832 | tf_op jit(solution)/shard_map/ks,qsc->kqc/dot_general | solution.py:32
  403.5 30.3 %reduce-scatter.14.cloned.1.call-done = f32[192,32]{1,0:T(8,128)} async-done(((f32[1536,32]{1,0:T(8,128)}), f32[192,32]{1,0:T(8,128)}) %reduce-scatter.14.cloned.1.call-update) | async-done | bytes 24592
  434.9 15.7 %all-gather.3 = f32[32,1,1536]{0,1,2:T(1,128)S(1)} all-gather(f32[32,1,192]{0,1,2:T(1,128)S(1)} %copy.21), channel_id=5, replica_groups=mesh['wide'=8,'narrow'=4] {'wide'}, dimensions={2}, use_global_device_ids=true | all-gather | bytes 221184 | tf_op jit(solution)/shard_map/all_gather | solution.py:26
  450.6 2.6 fusion.28
  (75 shorter events, 43.5 us)
Async XLA Ops:
  7.2 315.4 %reduce-scatter.10.cloned.1.call-start = ((), (), s32[]{:S(2)}) async-start(), calls=%async_computation.6 | async-start | bytes 884736
  121.6 1.3 copy-start
  122.9 36.9 %copy-start.2 = (f32[2,256,256]{2,1,0:T(8,128)S(1)}, f32[2,256,256]{2,1,0:T(8,128)}, u32[]{:S(2)}) copy-start(f32[2,256,256]{2,1,0:T(8,128)} %param.7) | copy-start | bytes 1572868
  233.2 1.3 copy-start.1
  293.1 85.7 %reduce-scatter.12.cloned.1.call-start = ((), (), s32[]{:S(2)}) async-start(), calls=%async_computation.7 | async-start | bytes 884736
  348.5 85.3 %reduce-scatter.14.cloned.1.call-start = ((), (), s32[]{:S(2)}) async-start(), calls=%async_computation.8 | async-start | bytes 884736
Sparse Core Ops, SparseCore 0:
  293.2 29.3 reduce-scatter.9
  348.6 30.1 reduce-scatter.11
  403.5 30.2 reduce-scatter.13
